TPU v7x, 32 devices: a whole 2x2x4 slice. The times are simulated.
32 devices in a mesh: sp: 16 (over z, x, core), tp: 2 (over y).
Axes of the slice: x: 2, y: 2, z: 4, core: 2. Of those that a mesh axis runs over, the one named last changes fastest.
Arguments:
- leak_rate: float32 [2, 32768, 1024], P(None, 'sp', 'tp'), may hold values from 0.2 to 2
- signal_in: bfloat16 [2, 32768, 1024], P(None, 'sp', 'tp'), may hold values from -6 to 6
- gate_in: bfloat16 [2, 32768, 1024], P(None, 'sp', 'tp'), may hold values from -6 to 6
Outputs:
- sequence_out: bfloat16 [2, 32768, 1024], P(None, 'sp', 'tp')
All inputs are finite; a program needn't handle non-finite values.
Results may differ from a plain program's by a relative error of at most 0.0017.
Values sent between devices are 32-bit elements; how exact they have to be, the bound alone decides.
A program may use at most 192 MiB of HBM per device.

v0:
```python
import functools
import math

import jax
import jax.numpy as jnp
from jax import lax
from jax.experimental import pallas as pl
from jax.experimental.pallas import tpu as pltpu
from jax.sharding import PartitionSpec as P

F32, BF16 = jnp.float32, jnp.bfloat16
VMEM = pltpu.VMEM
MIB = 1 << 20


def chunk_copy(hbm, vmem, sem, j, rows):
    at = pl.ds(pl.multiple_of(j * rows, rows), rows)
    return pltpu.make_async_copy(hbm.at[:, at, :], vmem.at[:, at, :], sem.at[j])


def local_kernel(
    total_length, rows, leak_hbm, signal_hbm, gate_hbm,
    mixed_ref, from_left_ref, from_right_ref, block_ref, message_ref,
    leak, signal, gate, leak_sem, signal_sem, gate_sem,
):
    batch, length, channels = leak.shape
    blocks = length // rows
    rate = math.log2(math.e) / total_length
    half_scale = 0.5 * total_length ** -0.5

    def start(j, _):
        chunk_copy(leak_hbm, leak, leak_sem, j, rows).start()
        chunk_copy(signal_hbm, signal, signal_sem, j, rows).start()
        chunk_copy(gate_hbm, gate, gate_sem, j, rows).start()
        return _

    lax.fori_loop(0, blocks, start, 0)

    row = lax.broadcasted_iota(jnp.int32, (rows, 2 * rows), 0)
    col = lax.broadcasted_iota(jnp.int32, (rows, 2 * rows), 1) % rows
    upto = jnp.where(row >= col, 1.0, 0.0).astype(BF16)
    onward = jnp.where(row <= col, 1.0, 0.0).astype(BF16)
    once = upto[:, :rows]

    def step(j, carry):
        chunk_copy(leak_hbm, leak, leak_sem, j, rows).wait()
        chunk_copy(signal_hbm, signal, signal_sem, j, rows).wait()
        chunk_copy(gate_hbm, gate, gate_sem, j, rows).wait()
        at = pl.ds(pl.multiple_of(j * rows, rows), rows)
        new = []
        for b in range(batch):
            lk = leak[b, at, :]
            x = signal[b, at, :]
            xf = x.astype(F32)
            upto_here = jnp.dot(once, lk.astype(BF16), preferred_element_type=F32) * rate
            before = upto_here - lk * rate
            low_f = ((jnp.exp2(upto_here) - 1.0) * xf).astype(BF16)
            low_b = ((jnp.exp2(-before) - 1.0) * xf).astype(BF16)
            sum_f = jnp.dot(upto, jnp.concatenate([x, low_f], 0), preferred_element_type=F32)
            sum_b = jnp.dot(onward, jnp.concatenate([x, low_b], 0), preferred_element_type=F32)
            u = jnp.exp2(-upto_here)
            v = jnp.exp2(before)
            gated = half_scale + half_scale * jnp.tanh(gate[b, at, :].astype(F32) * 0.5)
            fwd = u * sum_f
            bwd = v * sum_b
            mixed_ref[b, at, :] = (fwd + bwd) * gated
            from_left_ref[b, at, :] = u * gated
            from_right_ref[b, at, :] = v * gated
            leaked = jnp.sum(lk, axis=0, keepdims=True)
            end_f, end_b = fwd[rows - 1 :], bwd[:1]
            block_ref[j, pl.ds(b, 1), :] = leaked
            block_ref[j, pl.ds(batch + b, 1), :] = end_f
            block_ref[j, pl.ds(2 * batch + b, 1), :] = end_b
            all_leaked, all_f, all_b = carry[b]
            new.append((
                all_leaked + leaked,
                jnp.exp2(-rate * leaked) * all_f + end_f,
                all_b + jnp.exp2(-rate * all_leaked) * end_b,
            ))
        return tuple(new)

    zero = jnp.zeros((1, channels), F32)
    final = lax.fori_loop(0, blocks, step, ((zero, zero, zero),) * batch)
    for b in range(batch):
        all_leaked, all_f, all_b = final[b]
        message_ref[0, pl.ds(b, 1), :] = all_leaked
        message_ref[1, pl.ds(b, 1), :] = all_leaked
        message_ref[0, pl.ds(batch + b, 1), :] = all_f
        message_ref[1, pl.ds(batch + b, 1), :] = all_b


def exchange_kernel(total_length, n, message_ref, enter_ref, held, send_sem, recv_sem):
    me = lax.axis_index("sp")
    batch = message_ref.shape[1] // 2
    rate = math.log2(math.e) / total_length
    barrier = pltpu.get_barrier_semaphore()
    for d in range(1, n):
        pl.semaphore_signal(
            barrier, inc=1, device_id={"sp": lax.rem(me + d, n)}, device_id_type=pl.DeviceIdType.MESH
        )
    pl.semaphore_wait(barrier, n - 1)
    copies = []
    for d in range(1, n):
        side = jnp.where(me + d < n, 0, 1)
        copies.append(pltpu.make_async_remote_copy(
            src_ref=message_ref.at[side],
            dst_ref=held.at[d],
            send_sem=send_sem.at[d],
            recv_sem=recv_sem.at[d],
            device_id={"sp": lax.rem(me + d, n)},
            device_id_type=pl.DeviceIdType.MESH,
        ))
        copies[-1].start()
    for copy in copies:
        copy.wait()
    zero = jnp.zeros((batch,) + message_ref.shape[2:], F32)
    state_f, state_b, passed_f, passed_b = zero, zero, zero, zero
    for d in range(1, n):
        got = held[d]
        state_f = jnp.where(me >= d, state_f + jnp.exp2(-rate * passed_f) * got[batch:], state_f)
        passed_f = passed_f + got[:batch]
        got = held[n - d]
        state_b = jnp.where(me + d < n, state_b + jnp.exp2(-rate * passed_b) * got[batch:], state_b)
        passed_b = passed_b + got[:batch]
    enter_ref[0] = state_f
    enter_ref[1] = state_b


def finish_kernel(
    total_length, rows, mixed_ref, from_left_ref, from_right_ref, block_ref, enter_ref,
    out_hbm, out, left, right, out_sem,
):
    batch, length, channels = out.shape
    blocks = length // rows
    rate = math.log2(math.e) / total_length

    def carry(k, states):
        state_f, state_b = states
        left[k] = state_f
        state_f = jnp.exp2(-rate * block_ref[k, :batch]) * state_f + block_ref[k, batch : 2 * batch]
        j = blocks - 1 - k
        state_b = jnp.exp2(-rate * block_ref[j, :batch]) * state_b
        right[j] = state_b
        state_b = state_b + block_ref[j, 2 * batch : 3 * batch]
        return state_f, state_b

    lax.fori_loop(0, blocks, carry, (enter_ref[0], enter_ref[1]))

    def copy(j):
        at = pl.ds(pl.multiple_of(j * rows, rows), rows)
        return pltpu.make_async_copy(out.at[:, at, :], out_hbm.at[:, at, :], out_sem.at[j])

    def step(j, _):
        at = pl.ds(pl.multiple_of(j * rows, rows), rows)
        for b in range(batch):
            out[b, at, :] = (
                mixed_ref[b, at, :]
                + from_left_ref[b, at, :] * left[j, pl.ds(b, 1), :]
                + from_right_ref[b, at, :] * right[j, pl.ds(b, 1), :]
            ).astype(BF16)
        copy(j).start()
        return _

    lax.fori_loop(0, blocks, step, 0)

    def finish(j, _):
        copy(j).wait()
        return _

    lax.fori_loop(0, blocks, finish, 0)


def per_device(n, leak_rate, signal_in, gate_in):
    batch, length, channels = leak_rate.shape
    total_length = length * n
    rows = math.gcd(length, 128)
    blocks = length // rows
    shape = (batch, length, channels)
    whole = pl.BlockSpec(memory_space=VMEM)
    far = pl.BlockSpec(memory_space=pl.ANY)
    slab = VMEM(shape, F32)
    dma = pltpu.SemaphoreType.DMA
    mixed, from_left, from_right, block, message = pl.pallas_call(
        functools.partial(local_kernel, total_length, rows),
        out_shape=(
            slab, slab, slab,
            VMEM((blocks, -(-3 * batch // 8) * 8, channels), F32),
            VMEM((2, 2 * batch, channels), F32),
        ),
        in_specs=[far] * 3,
        out_specs=(whole,) * 5,
        scratch_shapes=[
            VMEM(shape, F32), VMEM(shape, BF16), VMEM(shape, BF16),
            dma((blocks,)), dma((blocks,)), dma((blocks,)),
        ],
        compiler_params=pltpu.CompilerParams(vmem_limit_bytes=26 * MIB),
        name="local",
    )(leak_rate, signal_in, gate_in)
    enter = pl.pallas_call(
        functools.partial(exchange_kernel, total_length, n),
        out_shape=VMEM((2, batch, channels), F32),
        in_specs=[whole],
        out_specs=whole,
        scratch_shapes=[VMEM((n, 2 * batch, channels), F32), dma((n,)), dma((n,))],
        compiler_params=pltpu.CompilerParams(
            collective_id=0, has_side_effects=True, vmem_limit_bytes=4 * MIB
        ),
        name="exchange",
    )(message)
    return pl.pallas_call(
        functools.partial(finish_kernel, total_length, rows),
        out_shape=jax.ShapeDtypeStruct(shape, BF16),
        in_specs=[whole] * 5,
        out_specs=far,
        scratch_shapes=[
            VMEM(shape, BF16), VMEM((blocks, batch, channels), F32),
            VMEM((blocks, batch, channels), F32), dma((blocks,)),
        ],
        compiler_params=pltpu.CompilerParams(vmem_limit_bytes=6 * MIB),
        name="finish",
    )(mixed, from_left, from_right, block, enter)


def solution(mesh):
    spec = P(None, "sp", "tp")
    return jax.shard_map(
        functools.partial(per_device, mesh.shape["sp"]),
        mesh=mesh,
        in_specs=(spec, spec, spec),
        out_specs=spec,
        check_vma=False,
    )
```

profile of v0, /device:TPU:0, one launch (start us, length us, event | category | flops | bytes accessed | tf_op | source)
XLA Modules:
  0.0 29.2 jit_solution(6330812631741976029)
XLA Ops:
  0.0 16.7 %local.1 = (f32[2,2048,512]{2,1,0:T(8,128)S(1)}, f32[2,2048,512]{2,1,0:T(8,128)S(1)}, f32[2,2048,512]{2,1,0:T(8,128)S(1)}, f32[16,8,512]{2,1,0:T(8,128)S(1)}, f32[2,4,512]{2,1,0:T(4,128)S(1)}) custom-call(f32[2,2048,512]{2,1,0:T(8,128)} %leak_hbm.1, bf16[2,2048,512]{2,1,0:T(8,128)(2,1)} %signal_hbm.1, bf16[2,2048,512]{2,1,0:T(8,128)(2,1)} %gate_hbm.1), custom_call_target="tpu_custom_call" | custom-call | tf_op jit(solution)/shard_map/local/pallas_call | solution.py:183
  16.7 9.5 %exchange.1.enter_ref = f32[2,2,512]{2,1,0:T(2,128)S(1)} custom-call(f32[2,4,512]{2,1,0:T(4,128)S(1)} %get-tuple-element.14.message_ref), custom_call_target="tpu_custom_call" | custom-call | tf_op jit(solution)/shard_map/exchange/pallas_call | solution.py:199
  26.2 3.1 %finish.1 = bf16[2,2048,512]{2,1,0:T(8,128)(2,1)} custom-call(f32[2,2048,512]{2,1,0:T(8,128)S(1)} %get-tuple-element.10.mixed_ref, f32[2,2048,512]{2,1,0:T(8,128)S(1)} %get-tuple-element.11.from_left_ref, f32[2,2048,512]{2,1,0:T(8,128)S(1)} %get-tuple-element.12.from_right_ref, f32[16,8,512]{2,1,0:T(8,128)S(1)} %get-tuple-element.13.block_ref, ...), custom_call_target="tpu_custom_call" | custom-call | tf_op jit(solution)/shard_map/finish/pallas_call | solution.py:210
where the time goes:
time: 29.4 us; the launch traced here: 29.2 us
  Pallas kernels  29.2 us (99%)
    pallas_call x1, Pallas kernels, per_device(): pl.pallas_call(functools.partial(local_kernel, total_length, rows), out_s...  16.7 us
    pallas_call x1, Pallas kernels, per_device(): pl.pallas_call(functools.partial(exchange_kernel, total_length, n), out_s...  9.49 us
    pallas_call x1, Pallas kernels, per_device(): pl.pallas_call(functools.partial(finish_kernel, total_length, rows), out_...  3.07 us

commit v1 on v0

v1 whole, which is shorter than its diff:
```python
import functools
import math

import jax
import jax.numpy as jnp
from jax import lax
from jax.experimental import pallas as pl
from jax.experimental.pallas import tpu as pltpu
from jax.sharding import PartitionSpec as P

F32, BF16 = jnp.float32, jnp.bfloat16
VMEM = pltpu.VMEM
MIB = 1 << 20


def chunk_copy(hbm, vmem, sem, j, rows):
    at = pl.ds(pl.multiple_of(j * rows, rows), rows)
    return pltpu.make_async_copy(hbm.at[:, at, :], vmem.at[:, at, :], sem.at[j])


def local_kernel(
    total_length, n, rows, cols, leak_hbm, signal_hbm, gate_hbm,
    mixed_ref, from_left_ref, from_right_ref, block_ref, enter_ref,
    leak, signal, gate, message, held, leak_sem, signal_sem, gate_sem, send_sem, recv_sem,
):
    batch, length, channels = leak.shape
    blocks = length // rows
    rate = math.log2(math.e) / total_length
    half_scale = 0.5 * total_length ** -0.5
    me = lax.axis_index("sp")
    barrier = pltpu.get_barrier_semaphore()

    def start(j, _):
        chunk_copy(leak_hbm, leak, leak_sem, j, rows).start()
        chunk_copy(signal_hbm, signal, signal_sem, j, rows).start()
        return _

    def start_gate(j, _):
        chunk_copy(gate_hbm, gate, gate_sem, j, rows).start()
        return _

    ahead = math.gcd(4, blocks)
    lax.fori_loop(0, ahead, start, 0)
    for d in range(1, n):
        pl.semaphore_signal(
            barrier, inc=1, device_id={"sp": lax.rem(me + d, n)}, device_id_type=pl.DeviceIdType.MESH
        )

    row = lax.broadcasted_iota(jnp.int32, (rows, 2 * rows), 0)
    col = lax.broadcasted_iota(jnp.int32, (rows, 2 * rows), 1) % rows
    upto = jnp.where(row >= col, 1.0, 0.0).astype(BF16)
    onward = jnp.where(row <= col, 1.0, 0.0).astype(BF16)
    once = upto[:, :rows]

    def step(j, _):
        @pl.when(j + ahead < blocks)
        def more():
            start(j + ahead, 0)

        @pl.when(j + ahead >= blocks)
        def more():
            for k in range(blocks // ahead):
                start_gate((j + ahead - blocks) * (blocks // ahead) + k, 0)

        chunk_copy(leak_hbm, leak, leak_sem, j, rows).wait()
        chunk_copy(signal_hbm, signal, signal_sem, j, rows).wait()
        at = pl.ds(pl.multiple_of(j * rows, rows), rows)
        pieces = [(b, pl.ds(p, cols)) for b in range(batch) for p in range(0, channels, cols)]
        for b, cs in pieces:
            x = signal[b, at, cs]
            xf = x.astype(F32)
            a = leak[b, at, cs] * rate
            upto_here = jnp.dot(once, a.astype(BF16), preferred_element_type=F32)
            before = upto_here - a
            low_f = ((jnp.exp2(upto_here) - 1.0) * xf).astype(BF16)
            low_b = ((jnp.exp2(a - upto_here) - 1.0) * xf).astype(BF16)
            u = jnp.exp2(-upto_here)
            v = jnp.exp2(before)
            from_left_ref[b, at, cs] = u
            from_right_ref[b, at, cs] = v
            sum_f = jnp.dot(upto, jnp.concatenate([x, low_f], 0), preferred_element_type=F32)
            sum_b = jnp.dot(onward, jnp.concatenate([x, low_b], 0), preferred_element_type=F32)
            mixed_ref[b, at, cs] = u * sum_f + v * sum_b
            block_ref[j, pl.ds(b, 1), cs] = jnp.sum(a, axis=0, keepdims=True)
            block_ref[j, pl.ds(batch + b, 1), cs] = u[rows - 1 :] * sum_f[rows - 1 :]
            block_ref[j, pl.ds(2 * batch + b, 1), cs] = v[:1] * sum_b[:1]
        return _

    lax.fori_loop(0, blocks, step, 0)

    def total(k, states):
        leaked, state_f, state_b = states
        here = block_ref[k, :batch]
        state_f = jnp.exp2(-here) * state_f + block_ref[k, batch : 2 * batch]
        state_b = state_b + jnp.exp2(-leaked) * block_ref[k, 2 * batch : 3 * batch]
        return leaked + here, state_f, state_b

    zero = jnp.zeros((batch, channels), F32)
    leaked, state_f, state_b = lax.fori_loop(0, blocks, total, (zero, zero, zero))
    message[0, :batch] = leaked
    message[1, :batch] = leaked
    message[0, batch:] = state_f
    message[1, batch:] = state_b

    pl.semaphore_wait(barrier, n - 1)
    copies = []
    for d in range(1, n):
        copies.append(pltpu.make_async_remote_copy(
            src_ref=message.at[jnp.where(me + d < n, 0, 1)],
            dst_ref=held.at[d],
            send_sem=send_sem.at[d],
            recv_sem=recv_sem.at[d],
            device_id={"sp": lax.rem(me + d, n)},
            device_id_type=pl.DeviceIdType.MESH,
        ))
        copies[-1].start()

    def apply_gate(j, _):
        chunk_copy(gate_hbm, gate, gate_sem, j, rows).wait()
        at = pl.ds(pl.multiple_of(j * rows, rows), rows)
        for b in range(batch):
            open_by = half_scale + half_scale * jnp.tanh((gate[b, at, :] * 0.5).astype(F32))
            mixed_ref[b, at, :] = mixed_ref[b, at, :] * open_by
            from_left_ref[b, at, :] = from_left_ref[b, at, :] * open_by
            from_right_ref[b, at, :] = from_right_ref[b, at, :] * open_by
        return _

    lax.fori_loop(0, blocks, apply_gate, 0)
    for copy in copies:
        copy.wait()
    state_f, state_b, passed_f, passed_b = zero, zero, zero, zero
    for d in range(1, n):
        got = held[d]
        state_f = jnp.where(me >= d, state_f + jnp.exp2(-passed_f) * got[batch:], state_f)
        passed_f = passed_f + got[:batch]
        got = held[n - d]
        state_b = jnp.where(me + d < n, state_b + jnp.exp2(-passed_b) * got[batch:], state_b)
        passed_b = passed_b + got[:batch]
    enter_ref[0] = state_f
    enter_ref[1] = state_b


def finish_kernel(
    rows, mixed_ref, from_left_ref, from_right_ref, block_ref, enter_ref,
    out_hbm, out, left, right, out_sem,
):
    batch, length, channels = out.shape
    blocks = length // rows

    def carry(k, states):
        state_f, state_b = states
        left[k] = state_f
        state_f = jnp.exp2(-block_ref[k, :batch]) * state_f + block_ref[k, batch : 2 * batch]
        j = blocks - 1 - k
        state_b = jnp.exp2(-block_ref[j, :batch]) * state_b
        right[j] = state_b
        state_b = state_b + block_ref[j, 2 * batch : 3 * batch]
        return state_f, state_b

    lax.fori_loop(0, blocks, carry, (enter_ref[0], enter_ref[1]))

    def copy(j):
        at = pl.ds(pl.multiple_of(j * rows, rows), rows)
        return pltpu.make_async_copy(out.at[:, at, :], out_hbm.at[:, at, :], out_sem.at[j])

    def step(j, _):
        at = pl.ds(pl.multiple_of(j * rows, rows), rows)
        for b in range(batch):
            out[b, at, :] = (
                mixed_ref[b, at, :]
                + from_left_ref[b, at, :] * left[j, pl.ds(b, 1), :]
                + from_right_ref[b, at, :] * right[j, pl.ds(b, 1), :]
            ).astype(BF16)
        copy(j).start()
        return _

    lax.fori_loop(0, blocks, step, 0)

    def finish(j, _):
        copy(j).wait()
        return _

    lax.fori_loop(0, blocks, finish, 0)


def per_device(n, leak_rate, signal_in, gate_in):
    batch, length, channels = leak_rate.shape
    total_length = length * n
    rows = math.gcd(length, 128)
    blocks = length // rows
    shape = (batch, length, channels)
    whole = pl.BlockSpec(memory_space=VMEM)
    far = pl.BlockSpec(memory_space=pl.ANY)
    slab = VMEM(shape, F32)
    dma = pltpu.SemaphoreType.DMA
    mixed, from_left, from_right, block, enter = pl.pallas_call(
        functools.partial(local_kernel, total_length, n, rows, channels),
        out_shape=(
            slab, slab, slab,
            VMEM((blocks, -(-3 * batch // 8) * 8, channels), F32),
            VMEM((2, batch, channels), F32),
        ),
        in_specs=[far] * 3,
        out_specs=(whole,) * 5,
        scratch_shapes=[
            VMEM(shape, F32), VMEM(shape, BF16), VMEM(shape, BF16),
            VMEM((2, 2 * batch, channels), F32), VMEM((n, 2 * batch, channels), F32),
            dma((blocks,)), dma((blocks,)), dma((blocks,)), dma((n,)), dma((n,)),
        ],
        compiler_params=pltpu.CompilerParams(
            collective_id=0, has_side_effects=True, vmem_limit_bytes=26 * MIB
        ),
        name="local",
    )(leak_rate, signal_in, gate_in)
    return pl.pallas_call(
        functools.partial(finish_kernel, rows),
        out_shape=jax.ShapeDtypeStruct(shape, BF16),
        in_specs=[whole] * 5,
        out_specs=far,
        scratch_shapes=[
            VMEM(shape, BF16), VMEM((blocks, batch, channels), F32),
            VMEM((blocks, batch, channels), F32), dma((blocks,)),
        ],
        compiler_params=pltpu.CompilerParams(vmem_limit_bytes=6 * MIB),
        name="finish",
    )(mixed, from_left, from_right, block, enter)


def solution(mesh):
    spec = P(None, "sp", "tp")
    return jax.shard_map(
        functools.partial(per_device, mesh.shape["sp"]),
        mesh=mesh,
        in_specs=(spec, spec, spec),
        out_specs=spec,
        check_vma=False,
    )
```

time: 29.4 us -> 26.6 us (0.905)
  Pallas kernels: 29.2 us -> 26.4 us
    pallas_call x3 -> x2, Pallas kernels: 29.2 us -> 26.4 us  [the longest x1 23.9 us: per_device(): pl.pallas_call(functools.partial(local_kernel, total_length, n, rows, cha...]
where the time goes in v1:
time: 26.6 us; the launch traced here: 26.4 us
  Pallas kernels  26.4 us (99%)
    pallas_call x1, Pallas kernels, per_device(): pl.pallas_call(functools.partial(local_kernel, total_length, n, rows, cha...  23.9 us
    pallas_call x1, Pallas kernels, per_device(): pl.pallas_call(functools.partial(finish_kernel, rows), out_shape=jax.Shap...  2.49 us

profile of v1, /device:TPU:0, one launch (start us, length us, event | category | flops | bytes accessed | tf_op | source)
XLA Modules:
  0.0 26.4 jit_solution(2537263205895209488)
XLA Ops:
  0.0 23.9 %local.1 = (f32[2,2048,512]{2,1,0:T(8,128)S(1)}, f32[2,2048,512]{2,1,0:T(8,128)S(1)}, f32[2,2048,512]{2,1,0:T(8,128)S(1)}, f32[16,8,512]{2,1,0:T(8,128)S(1)}, f32[2,2,512]{2,1,0:T(2,128)S(1)}) custom-call(f32[2,2048,512]{2,1,0:T(8,128)} %leak_hbm.1, bf16[2,2048,512]{2,1,0:T(8,128)(2,1)} %signal_hbm.1, bf16[2,2048,512]{2,1,0:T(8,128)(2,1)} %gate_hbm.1), custom_call_target="tpu_custom_call" | custom-call | tf_op jit(solution)/shard_map/local/pallas_call | solution.py:196
  23.9 2.5 %finish.1 = bf16[2,2048,512]{2,1,0:T(8,128)(2,1)} custom-call(f32[2,2048,512]{2,1,0:T(8,128)S(1)} %get-tuple-element.10.mixed_ref, f32[2,2048,512]{2,1,0:T(8,128)S(1)} %get-tuple-element.11.from_left_ref, f32[2,2048,512]{2,1,0:T(8,128)S(1)} %get-tuple-element.12.from_right_ref, f32[16,8,512]{2,1,0:T(8,128)S(1)} %get-tuple-element.13.block_ref, ...), custom_call_target="tpu_custom_call" | custom-call | tf_op jit(solution)/shard_map/finish/pallas_call | solution.py:215
